TPU v7x, 32 devices: a whole 2x2x4 slice. The times are simulated.
32 devices in a mesh: seq: 8 (over z, x), head: 4 (over y, core).
Axes of the slice: x: 2, y: 2, z: 4, core: 2. Of those that a mesh axis runs over, the one named last changes fastest.
Arguments:
- queries: bfloat16 [2048, 64, 128], P('seq', 'head'), may hold values from -360 to 360
- head_weights: bfloat16 [2048, 64], P('seq', 'head'), may hold values from -0.75 to 0.75
- keys: bfloat16 [2048, 128], P('seq'), may hold values from -6 to 6
- targets: bfloat16 [2048, 2048], P('seq'), may hold values from 0.0099487305 to 10
- chosen: int32 [16, 16], P('seq'), may hold values from -1 to 15, as said below
- tile_block: int32 [16], replicated, may hold values from 0 to 15, as said below
Outputs:
- query_grads: bfloat16 [2048, 64, 128], P('seq', 'head')
- weight_grads: float32 [2048, 64], P('seq', 'head')
- key_grads: float32 [2048, 128], P('seq')
- loss: float32 [], replicated
Inputs may be any that keep to these rules, and one draw needn't show every extreme that they name: `tile_block`: a permutation of 0 to 15; each aligned group of 4 stored positions holds the global blocks of that same group. `chosen`: slot 0 of stored tile p is tile_block[p]; live entries of a row are distinct, none exceeds tile_block[p], and they precede the -1 entries; over all tiles of one device of seq, at most 1 distinct live block is stored on any one other device.
All inputs are finite; a program needn't handle non-finite values.
Results may differ from a plain program's by a relative error of at most 0.0095.
Values may be sent and summed in bfloat16 or wider, within the bound.
No kernel may reach another device: no remote copies, remote signals or barrier semaphores. Data moves between devices by JAX's collectives and lax.ppermute only.
A program may use at most 128 MiB of HBM per device.

v0:
```python
import jax
import jax.numpy as jnp
from jax import lax
from jax.sharding import PartitionSpec as P

BLOCK = 128
SLOTS = 16
CAP = 1
KEYS = 2048
loss_scale = 4194304.0


def row_statistics(score_part, mask_part, target_part):
    row_max = jnp.max(jnp.where(mask_part, score_part, -1e30), axis=1)
    exp_terms = jnp.where(
        mask_part, jnp.exp(jnp.where(mask_part, score_part - row_max[:, None], 0.0)), 0.0
    )
    return (row_max, jnp.sum(exp_terms, axis=1), jnp.sum(target_part, axis=1))


def local(queries, head_weights, keys, targets, chosen, tile_block):
    row_count, heads_here, key_width = queries.shape
    tiles_here = row_count // BLOCK
    block_count = tile_block.shape[0]
    owner_count = block_count // tiles_here
    score_scale = key_width ** (-0.5)
    seq_index = lax.axis_index("seq")
    head_index = lax.axis_index("head")
    is_first = (head_index == 0).astype(jnp.float32)
    positions = jnp.arange(block_count, dtype=jnp.int32)
    home_of = jnp.sum(
        jnp.where(tile_block[None, :] == positions[:, None], positions[None, :], 0), axis=1
    )
    live_slot = chosen >= 0
    position = home_of[jnp.maximum(chosen, 0)]
    owner_index = position // tiles_here
    local_slot = position % tiles_here
    own_block = lax.dynamic_slice_in_dim(tile_block, seq_index * tiles_here, tiles_here)
    offsets = jnp.arange(BLOCK, dtype=jnp.int32)
    causal = offsets[None, :] <= offsets[:, None]
    own_slot = chosen == own_block[:, None]
    live_mask = live_slot[:, None, :, None] & (
        (~own_slot)[:, None, :, None] | causal[None, :, None, :]
    )
    live_mask = live_mask.reshape(row_count, KEYS)
    key_blocks = keys.reshape(tiles_here, BLOCK, key_width)
    remote = live_slot & (owner_index != seq_index)
    remote_pos = jnp.where(remote, position, -1).reshape(-1)
    wanted = jnp.any(remote_pos[:, None] == positions[None, :], axis=0).reshape(
        owner_count, tiles_here
    )
    slot_rank = jnp.cumsum(wanted.astype(jnp.int32), axis=1) - 1
    local_iota = jnp.arange(tiles_here, dtype=jnp.int32)
    request = jnp.stack(
        [jnp.sum(jnp.where(wanted & (slot_rank == 0), local_iota[None, :], 0), axis=1)], axis=1
    )
    asked_slots = lax.all_to_all(request, "seq", split_axis=0, concat_axis=0, tiled=True)
    reply_blocks = key_blocks[asked_slots]
    arrived = lax.all_to_all(reply_blocks, "seq", split_axis=0, concat_axis=0, tiled=True)
    key_table = jnp.concatenate(
        [key_blocks, arrived.reshape(owner_count * CAP, BLOCK, key_width)], axis=0
    )
    table_index = jnp.where(
        owner_index == seq_index,
        local_slot,
        tiles_here + owner_index * CAP + slot_rank[owner_index, local_slot],
    )
    table_index = jnp.where(live_slot, table_index, 0)
    fetched = key_table[table_index]
    query_tiles = queries.reshape(tiles_here, BLOCK, heads_here, key_width)
    weight_tiles = head_weights.astype(jnp.float32).reshape(tiles_here, BLOCK, heads_here)

    def dot_values(query_tile, key_tile):
        return jnp.einsum(
            "qhd,kd->qhk",
            query_tile,
            key_tile.reshape(-1, key_width),
            preferred_element_type=jnp.float32,
        )

    def forward(operands):
        query_tile, weight_tile, key_tile = operands
        values = dot_values(query_tile, key_tile)
        return score_scale * jnp.sum(jnp.maximum(values, 0.0) * weight_tile[:, :, None], axis=1)

    partial_value = lax.map(forward, (query_tiles, weight_tiles, fetched)).reshape(row_count, KEYS)
    target_vals = jnp.where(live_mask, targets.astype(jnp.float32), 0.0)
    pair_local = jnp.sum(live_mask.astype(jnp.float32))
    score_part = lax.psum(partial_value, "head")
    row_max, row_norm, row_target = row_statistics(score_part, live_mask, target_vals)
    target_prob = jnp.where(live_mask, target_vals / row_target[:, None], 0.0)
    kl_cols = jnp.sum(
        jnp.where(
            live_mask,
            target_prob * (jnp.log(jnp.where(live_mask, target_prob, 1.0)) - score_part),
            0.0,
        )
    )
    lse_sum = jnp.sum(row_max + jnp.log(row_norm))
    loss_part = is_first * (kl_cols + lse_sum)
    loss_total, pair_count = lax.psum((loss_part, is_first * pair_local), ("seq", "head"))
    softmax_vals = (
        jnp.where(live_mask, jnp.exp(jnp.where(live_mask, score_part - row_max[:, None], 0.0)), 0.0)
        / row_norm[:, None]
    )
    grad_part = loss_scale * KEYS * (softmax_vals - target_prob) / pair_count
    grad_tiles = grad_part.reshape(tiles_here, BLOCK, KEYS)

    def backward(operands):
        query_tile, weight_tile, key_tile, grad_tile = operands
        key_rows = key_tile.reshape(-1, key_width)
        values = dot_values(query_tile, key_tile)
        weight_grad = score_scale * jnp.sum(
            jnp.maximum(values, 0.0) * grad_tile[:, None, :], axis=2
        )
        dot_grads = (
            score_scale
            * weight_tile[:, :, None]
            * grad_tile[:, None, :]
            * (values > 0).astype(jnp.float32)
        ).astype(jnp.bfloat16)
        query_grad = jnp.einsum(
            "qhk,kd->qhd", dot_grads, key_rows, preferred_element_type=jnp.float32
        ).astype(jnp.bfloat16)
        key_grad = jnp.einsum(
            "qhk,qhd->kd", dot_grads, query_tile, preferred_element_type=jnp.float32
        )
        return (query_grad, weight_grad, key_grad.reshape(SLOTS, BLOCK, key_width))

    query_grads, weight_grads, key_parts = lax.map(
        backward, (query_tiles, weight_tiles, fetched, grad_tiles)
    )
    slot_grads = key_parts.reshape(tiles_here * SLOTS, BLOCK, key_width)
    spread = jax.ops.segment_sum(
        slot_grads, table_index.reshape(-1), num_segments=tiles_here + owner_count * CAP
    )
    returned = lax.all_to_all(
        spread[tiles_here:].reshape(owner_count, CAP, BLOCK, key_width).astype(jnp.bfloat16),
        "seq",
        split_axis=0,
        concat_axis=0,
        tiled=True,
    ).astype(jnp.float32)
    owned_grad = spread[:tiles_here] + jax.ops.segment_sum(
        returned.reshape(owner_count * CAP, BLOCK, key_width),
        asked_slots.reshape(-1),
        num_segments=tiles_here,
    )
    key_grads = lax.psum(owned_grad.astype(jnp.bfloat16), "head").astype(jnp.float32)
    return (
        query_grads.reshape(row_count, heads_here, key_width),
        weight_grads.reshape(row_count, heads_here),
        key_grads.reshape(row_count, key_width),
        KEYS * loss_total / pair_count,
    )


def solution(mesh):
    placed = (
        P("seq", "head", None),
        P("seq", "head"),
        P("seq", None),
        P("seq", None),
        P("seq", None),
        P(),
    )
    return jax.shard_map(
        local,
        mesh=mesh,
        in_specs=placed,
        out_specs=(P("seq", "head", None), P("seq", "head"), P("seq", None), P()),
        check_vma=False,
    )
```

profile of v0, /device:TPU:0, one launch (start us, length us, event | category | flops | bytes accessed | tf_op | source)
XLA Modules:
  0.0 263.6 jit_solution(3088929878997966264)
XLA Ops:
  7.2 0.8 select_reduce_fusion.2
  7.9 0.7 broadcast_maximum_fusion
  8.7 0.7 gather_fusion
  9.5 0.7 and_select_fusion.3
  10.8 0.7 copy.39
  11.5 7.3 %all-to-all-start = ((s32[8,1,1]{2,1,0:T(1,128)}), s32[8,1,1]{2,1,0:T(1,128)S(1)}, u32[]{:S(2)}, u32[]{:S(2)}) async-start(s32[8,1,1]{2,1,0:T(1,128)} %copy.39), calls=%async_computation | async-start | bytes 8192 | tf_op jit(solution)/shard_map/all_to_all | solution.py:57
  18.8 1.5 copy.42
  20.4 0.7 gather_fusion.2
  21.2 4.0 %all-to-all-done = s32[8,1,1]{2,1,0:T(1,128)S(1)} async-done(((s32[8,1,1]{2,1,0:T(1,128)}), s32[8,1,1]{2,1,0:T(1,128)S(1)}, u32[]{:S(2)}, u32[]{:S(2)}) %all-to-all-start) | async-done | bytes 64 | tf_op jit(solution)/shard_map/all_to_all | solution.py:57
  25.2 0.7 fusion.46
  25.9 1.3 gather_fusion.1
  27.2 3.4 %all-to-all-start.1 = ((bf16[8,1,128,128]{3,2,1,0:T(8,128)(2,1)}), bf16[8,1,128,128]{3,2,1,0:T(8,128)(2,1)S(1)}, u32[]{:S(2)}, u32[]{:S(2)}) async-start(bf16[8,1,128,128]{3,2,1,0:T(8,128)(2,1)} %bitcast.22), calls=%async_computation.1 | async-start | bytes 524288 | tf_op jit(solution)/shard_map/all_to_all | solution.py:59
  30.8 8.0 %all-to-all-done.1 = bf16[8,1,128,128]{3,2,1,0:T(8,128)(2,1)S(1)} async-done(((bf16[8,1,128,128]{3,2,1,0:T(8,128)(2,1)}), bf16[8,1,128,128]{3,2,1,0:T(8,128)(2,1)S(1)}, u32[]{:S(2)}, u32[]{:S(2)}) %all-to-all-start.1) | async-done | bytes 262176 | tf_op jit(solution)/shard_map/all_to_all | solution.py:59
  38.8 0.7 gather_fusion.3
  39.6 8.3 %while.24 = (s32[]{:T(128)}, f32[2,128,2048]{2,1,0:T(8,128)}, bf16[2,128,16,128]{3,1,2,0:T(8,128)(2,1)S(1)}, bf16[2,16,128,128]{3,2,1,0:T(8,128)(2,1)S(1)}, f32[2,128,16]{1,2,0:T(8,128)S(1)}, /*index=5*/s32[]{:T(128)}) while((s32[]{:T(128)}, f32[2,128,2048]{2,1,0:T(8,128)}, bf16[2,128,16,128]{3,1,2,0:T(8,128)(2,1)S(1)}, ...), condition=%wide.region_6.7_spmd, body=%wide.region_4.6_spmd.sunk | while | flops 1086324736 | bytes 22044820 | solution.py:86
  39.7 2.6 %multiply_reduce_fusion.4 = f32[128,2048]{1,0:T(8,128)S(1)} fusion(f32[128,16]{0,1:T(8,128)S(1)} %dynamic-slice_bitcast_fusion.5, bf16[2048,128,1]{1,0,2:T(8,128)(2,1)S(1)} %bitcast.151, bf16[2,128,16,128]{3,1,2,0:T(8,128)(2,1)S(1)} %get-tuple-element.283, s32[]{:T(128)S(6)} %copy.90), kind=kOutput, calls=%fused_computation.6.clone.1 | convolution fusion | flops 1086062592 | bytes 2105348 | tf_op jit(solution)/shard_map/while/body/eval_jaxpr/qhd,kd->qhk/dot_general | solution.py:74
  42.4 1.3 copy-done.6
  43.8 2.6 %multiply_reduce_fusion.4 = f32[128,2048]{1,0:T(8,128)S(1)} fusion(f32[128,16]{0,1:T(8,128)S(1)} %dynamic-slice_bitcast_fusion.5, bf16[2048,128,1]{1,0,2:T(8,128)(2,1)S(1)} %bitcast.151, bf16[2,128,16,128]{3,1,2,0:T(8,128)(2,1)S(1)} %get-tuple-element.283, s32[]{:T(128)S(6)} %copy.90), kind=kOutput, calls=%fused_computation.6.clone.1 | convolution fusion | flops 1086062592 | bytes 2105348 | tf_op jit(solution)/shard_map/while/body/eval_jaxpr/qhd,kd->qhk/dot_general | solution.py:74
  46.6 1.3 copy-done.6
  48.7 1.3 convert_reduce_fusion
  50.6 1.2 or_and_fusion
  51.8 46.2 %all-reduce.4.cloned.1.call-done = f32[256,2048]{1,0:T(8,128)} async-done(((f32[256,2048]{1,0:T(8,128)}), f32[256,2048]{1,0:T(8,128)}) %all-reduce.4.cloned.1.call-update) | async-done | bytes 2097168 | tf_op jit(solution)/shard_map/psum | solution.py:89
  98.0 2.9 %select_reduce_fusion.1 = (f32[256]{0:T(256)S(1)}, f32[256]{0:T(256)S(1)}) fusion(f32[256,2048]{1,0:T(8,128)} %all-reduce.4.cloned.1.call-done, pred[32,8,16,128]{3,2,1,0:T(8,128)(4,1)} %bitcast.152, bf16[256,2048]{1,0:T(8,128)(2,1)} %param.13), kind=kLoop, calls=%fused_computation.55 | loop fusion | flops 2620928 | bytes 3672064 | tf_op jit(solution)/shard_map/reduce_max | solution.py:14
  100.9 3.6 %select_reduce_fusion = (f32[]{:T(128)}, f32[256]{0:T(256)S(1)}) fusion(f32[256,2048]{1,0:T(8,128)S(1)} %copy-done, bf16[256,2048]{1,0:T(8,128)(2,1)} %param.13, f32[256]{0:T(256)S(1)} %get-tuple-element.134, pred[32,8,16,128]{3,2,1,0:T(8,128)(4,1)S(1)} %bitcast.154, f32[256]{0:T(256)S(1)} %get-tuple-element.133), kind=kLoop, calls=%fused_computation.48 | loop fusion | flops 6815487 | bytes 3673092 | tf_op jit(solution)/shard_map/reduce_sum | solution.py:92
  104.5 0.7 add_reduce_fusion
  107.1 39.5 %all-reduce = (f32[]{:T(128)}, f32[]{:T(128)}) all-reduce(f32[]{:T(128)S(6)} %mul.105, f32[]{:T(128)S(6)} %mul.107), channel_id=1, replica_groups=mesh['seq'=8,'head'=4] {'seq','head'}, use_global_device_ids=true, to_apply=%region_12.13 | all-reduce | flops 2 | bytes 16 | tf_op jit(solution)/shard_map/psum | solution.py:101
  146.6 4.7 %multiply_divide_fusion = f32[256,2048]{1,0:T(8,128)} fusion(f32[256,2048]{1,0:T(8,128)S(1)} %copy-done, bf16[256,2048]{1,0:T(8,128)(2,1)} %param.13, f32[]{:T(128)} %get-tuple-element.163, f32[256]{0:T(256)S(1)} %get-tuple-element.134, f32[256]{0:T(256)S(1)} %get-tuple-element.132, f32[256]{0:T(256)S(1)} %get-tuple-element.133, ...), kind=kLoop, calls=%fused_computation.50 | loop fusion | flops 5767168 | bytes 5770244 | tf_op jit(solution)/shard_map/div | solution.py:106
  151.4 51.8 %while.25 = (s32[]{:T(128)}, bf16[2,128,16,128]{3,2,1,0:T(8,128)(2,1)}, f32[2,128,16]{1,0,2:T(2,128)S(1)}, f32[2,16,128,128]{3,2,1,0:T(8,128)}, bf16[2,128,16,12...) while((s32[]{:T(128)}, ...), condition=%wide.region_15.16_spmd, body=%wide.region_13.15_spmd.sunk | while | flops 3313502208 | bytes 61949172 | solution.py:130
  151.4 1.6 dynamic-slice_bitcast_fusion.6
  153.1 7.1 %fusion.74 = (u16[128,2048]{1,0:T(8,128)(2,1)S(1)}, f32[128,16,2048]{2,0,1:T(8,128)}) fusion(bf16[2048,128,1]{1,0,2:T(8,128)(2,1)S(1)} %bitcast.147, bf16[2,128,16,128]{3,1,2,0:T(8,128)(2,1)S(1)} %copy-done.3, s32[]{:T(128)S(6)} %copy.99), kind=kOutput, calls=%fused_computation.21.clone.1 | convolution fusion | flops 1094451200 | bytes 18350084 | tf_op jit(solution)/shard_map/while/body/eval_jaxpr/qhd,kd->qhk/dot_general | solution.py:74
  160.2 2.7 %fusion.75 = bf16[1,128,16,128]{3,1,2,0:T(8,128)(2,1)S(1)} fusion(bf16[2048,128,1]{1,0,2:T(8,128)(2,1)S(1)} %bitcast.148, f32[128,2048]{1,0:T(8,128)S(1)} %get-tuple-element.263, f32[128,16]{0,1:T(8,128)S(1)} %get-tuple-element.264, u16[128,2048]{1,0:T(8,128)(2,1)S(1)} %get-tuple-element.265), kind=kOutput, calls=%fused_computation.30.clone.1 | convolution fusion | flops 1103364096 | bytes 2629632 | tf_op jit(solution)/shard_map/while/body/eval_jaxpr/qhk,kd->qhd/dot_general | solution.py:122
  163.3 1.0 copy-done.13
  164.3 7.5 %multiply_reduce_fusion.5 = f32[128,16]{0,1:T(8,128)S(1)} fusion(f32[128,16,2048]{2,0,1:T(8,128)} %get-tuple-element.266, f32[128,2048]{1,0:T(8,128)S(1)} %get-tuple-element.263), kind=kLoop, calls=%fused_computation.19.clone.1 | loop fusion | flops 12580864 | bytes 17833984 | tf_op jit(solution)/shard_map/while/body/eval_jaxpr/reduce_sum | solution.py:113
  171.8 5.4 %fusion.76 = f32[2,16,128,128]{3,2,1,0:T(8,128)} fusion(f32[2,16,128,128]{3,2,1,0:T(8,128)} %get-tuple-element.300, s32[]{:T(128)S(6)} %copy.99, bf16[2,128,16,128]{3,1,2,0:T(8,128)(2,1)} %get-tuple-element.311, f32[2048,128]{0,1:T(8,128)S(1)} %get-tuple-element.267, f32[16,128]{1,0:T(8,128)S(1)} %get-tuple-element.268, u16[128,2048]{1,0:T(8,128)(2,1)} %copy-done.1), kind=kOutput, calls=%fused_computation.28.clone.1 | convolution fusion | flops 1103101952 | bytes 3154944 | tf_op jit(solution)/shard_map/while/body/eval_jaxpr/qhk,qhd->kd/dot_general | solution.py:125
  177.3 1.6 dynamic-slice_bitcast_fusion.6
  178.9 7.1 %fusion.74 = (u16[128,2048]{1,0:T(8,128)(2,1)S(1)}, f32[128,16,2048]{2,0,1:T(8,128)}) fusion(bf16[2048,128,1]{1,0,2:T(8,128)(2,1)S(1)} %bitcast.147, bf16[2,128,16,128]{3,1,2,0:T(8,128)(2,1)S(1)} %copy-done.3, s32[]{:T(128)S(6)} %copy.99), kind=kOutput, calls=%fused_computation.21.clone.1 | convolution fusion | flops 1094451200 | bytes 18350084 | tf_op jit(solution)/shard_map/while/body/eval_jaxpr/qhd,kd->qhk/dot_general | solution.py:74
  186.1 2.7 %fusion.75 = bf16[1,128,16,128]{3,1,2,0:T(8,128)(2,1)S(1)} fusion(bf16[2048,128,1]{1,0,2:T(8,128)(2,1)S(1)} %bitcast.148, f32[128,2048]{1,0:T(8,128)S(1)} %get-tuple-element.263, f32[128,16]{0,1:T(8,128)S(1)} %get-tuple-element.264, u16[128,2048]{1,0:T(8,128)(2,1)S(1)} %get-tuple-element.265), kind=kOutput, calls=%fused_computation.30.clone.1 | convolution fusion | flops 1103364096 | bytes 2629632 | tf_op jit(solution)/shard_map/while/body/eval_jaxpr/qhk,kd->qhd/dot_general | solution.py:122
  189.2 1.0 copy-done.13
  190.2 7.5 %multiply_reduce_fusion.5 = f32[128,16]{0,1:T(8,128)S(1)} fusion(f32[128,16,2048]{2,0,1:T(8,128)} %get-tuple-element.266, f32[128,2048]{1,0:T(8,128)S(1)} %get-tuple-element.263), kind=kLoop, calls=%fused_computation.19.clone.1 | loop fusion | flops 12580864 | bytes 17833984 | tf_op jit(solution)/shard_map/while/body/eval_jaxpr/reduce_sum | solution.py:113
  197.7 5.4 %fusion.76 = f32[2,16,128,128]{3,2,1,0:T(8,128)} fusion(f32[2,16,128,128]{3,2,1,0:T(8,128)} %get-tuple-element.300, s32[]{:T(128)S(6)} %copy.99, bf16[2,128,16,128]{3,1,2,0:T(8,128)(2,1)} %get-tuple-element.311, f32[2048,128]{0,1:T(8,128)S(1)} %get-tuple-element.267, f32[16,128]{1,0:T(8,128)S(1)} %get-tuple-element.268, u16[128,2048]{1,0:T(8,128)(2,1)} %copy-done.1), kind=kOutput, calls=%fused_computation.28.clone.1 | convolution fusion | flops 1103101952 | bytes 3154944 | tf_op jit(solution)/shard_map/while/body/eval_jaxpr/qhk,qhd->kd/dot_general | solution.py:125
  203.2 4.7 %scatter_fusion = f32[10,128,128]{2,1,0:T(8,128)S(1)} fusion(f32[10,128,128]{2,1,0:T(8,128)S(1)} %broadcast_in_dim.106, s32[32]{0:T(128)S(1)} %copy-done.11, f32[32,128,128]{2,1,0:T(8,128)} %bitcast.155), kind=kCustom, calls=%fused_computation.4 | custom fusion | flops 524288 | bytes 6291584 | tf_op jit(solution)/shard_map/scatter-add | solution.py:134
  207.9 0.7 fusion.39
  208.6 5.3 %all-to-all-start.2 = ((bf16[8,1,128,128]{3,2,1,0:T(8,128)(2,1)}), bf16[8,1,128,128]{3,2,1,0:T(8,128)(2,1)S(1)}, u32[]{:S(2)}, u32[]{:S(2)}) async-start(bf16[8,1,128,128]{3,2,1,0:T(8,128)(2,1)} %fusion.39), calls=%async_computation.2 | async-start | bytes 524288 | tf_op jit(solution)/shard_map/all_to_all | solution.py:137
  213.9 8.4 %all-to-all-done.2 = bf16[8,1,128,128]{3,2,1,0:T(8,128)(2,1)S(1)} async-done(((bf16[8,1,128,128]{3,2,1,0:T(8,128)(2,1)}), bf16[8,1,128,128]{3,2,1,0:T(8,128)(2,1)S(1)}, u32[]{:S(2)}, u32[]{:S(2)}) %all-to-all-start.2) | async-done | bytes 262176 | tf_op jit(solution)/shard_map/all_to_all | solution.py:137
  222.4 1.0 scatter_fusion.1
  223.5 0.6 convert_element_type.35
  226.0 28.0 %all-reduce.6.cloned.1.call-done = bf16[256,128]{1,0:T(8,128)(2,1)} async-done(((bf16[256,128]{1,0:T(8,128)(2,1)}), bf16[256,128]{1,0:T(8,128)(2,1)}) %all-reduce.6.cloned.1.call-update) | async-done | bytes 65552 | tf_op jit(solution)/shard_map/psum | solution.py:149
  254.1 1.5 reshape.246
  (89 shorter events, 4.7 us)
Async XLA Ops:
  8.7 17.2 %copy-start.7 = (bf16[256,128]{1,0:T(8,128)(2,1)S(1)}, bf16[256,128]{1,0:T(8,128)(2,1)}, u32[]{:S(2)}) copy-start(bf16[256,128]{1,0:T(8,128)(2,1)} %param.12) | copy-start | bytes 196612
  11.5 13.7 %all-to-all-start = ((s32[8,1,1]{2,1,0:T(1,128)}), s32[8,1,1]{2,1,0:T(1,128)S(1)}, u32[]{:S(2)}, u32[]{:S(2)}) async-start(s32[8,1,1]{2,1,0:T(1,128)} %copy.39), calls=%async_computation | async-start | bytes 8192 | tf_op jit(solution)/shard_map/all_to_all | solution.py:57
  18.8 12.0 %copy-start.9 = (bf16[256,16]{0,1:T(8,128)(2,1)S(1)}, bf16[256,16]{0,1:T(8,128)(2,1)}, u32[]{:S(2)}) copy-start(bf16[256,16]{0,1:T(8,128)(2,1)} %param.11) | copy-start | bytes 24580
  27.2 11.6 %all-to-all-start.1 = ((bf16[8,1,128,128]{3,2,1,0:T(8,128)(2,1)}), bf16[8,1,128,128]{3,2,1,0:T(8,128)(2,1)S(1)}, u32[]{:S(2)}, u32[]{:S(2)}) async-start(bf16[8,1,128,128]{3,2,1,0:T(8,128)(2,1)} %bitcast.22), calls=%async_computation.1 | async-start | bytes 524288 | tf_op jit(solution)/shard_map/all_to_all | solution.py:59
  30.6 67.3 %all-reduce.4.cloned.1.call-start = ((), (), s32[]{:S(2)}) async-start(), calls=%async_computation.3 | async-start | bytes 4194304 | tf_op jit(solution)/shard_map/psum | solution.py:89
  39.6 2.7 %copy-start.5 = (f32[2,128,2048]{2,1,0:T(8,128)S(1)}, f32[2,128,2048]{2,1,0:T(8,128)}, u32[]{:S(2)}) copy-start(f32[2,128,2048]{2,1,0:T(8,128)} %get-tuple-element.276) | copy-start | bytes 6291460 | tf_op jit(solution)/shard_map/while
  42.4 1.3 copy-start.6
  43.8 2.7 %copy-start.5 = (f32[2,128,2048]{2,1,0:T(8,128)S(1)}, f32[2,128,2048]{2,1,0:T(8,128)}, u32[]{:S(2)}) copy-start(f32[2,128,2048]{2,1,0:T(8,128)} %get-tuple-element.276) | copy-start | bytes 6291460 | tf_op jit(solution)/shard_map/while
  46.6 1.3 copy-start.6
  47.9 3.9 %copy-start.2 = (bf16[2,128,16,128]{3,1,2,0:T(8,128)(2,1)}, bf16[2,128,16,128]{3,1,2,0:T(8,128)(2,1)S(1)}, u32[]{:S(2)}) copy-start(bf16[2,128,16,128]{3,1,2,0:T(8,128)(2,1)S(1)} %get-tuple-element.321) | copy-start | bytes 3145732
  47.9 0.7 copy-start.14
  47.9 0.7 copy-start.8
  98.0 2.9 %copy-start = (f32[256,2048]{1,0:T(8,128)S(1)}, f32[256,2048]{1,0:T(8,128)}, u32[]{:S(2)}) copy-start(f32[256,2048]{1,0:T(8,128)} %all-reduce.4.cloned.1.call-done) | copy-start | bytes 6291460
  98.0 2.9 %copy-start.4 = (pred[2,128,16,128]{3,2,1,0:T(8,128)(4,1)S(1)}, pred[2,128,16,128]{3,2,1,0:T(8,128)(4,1)}, u32[]{:S(2)}) copy-start(pred[2,128,16,128]{3,2,1,0:T(8,128)(4,1)} %or_and_fusion) | copy-start | bytes 1572868
  151.4 51.8 %copy-start.11 = (s32[32]{0:T(128)S(1)}, s32[32]{0:T(128)}, u32[]{:S(2)}) copy-start(s32[32]{0:T(128)} %reshape.283) | copy-start | bytes 388
  151.4 1.7 copy-start.3
  160.2 2.7 %copy-start.1 = (u16[128,2048]{1,0:T(8,128)(2,1)}, u16[128,2048]{1,0:T(8,128)(2,1)S(1)}, u32[]{:S(2)}) copy-start(u16[128,2048]{1,0:T(8,128)(2,1)S(1)} %get-tuple-element.265) | copy-start | bytes 1572868 | tf_op jit(solution)/shard_map/while
  160.2 2.7 %copy-start.12 = (bf16[2,128,16,128]{3,2,1,0:T(8,128)(2,1)S(1)}, bf16[2,128,16,128]{3,2,1,0:T(8,128)(2,1)}, u32[]{:S(2)}) copy-start(bf16[2,128,16,128]{3,2,1,0:T(8,128)(2,1)} %get-tuple-element.298) | copy-start | bytes 3145732 | tf_op jit(solution)/shard_map/while
  163.3 1.0 copy-start.13
  177.3 1.7 copy-start.3
  186.1 2.7 %copy-start.1 = (u16[128,2048]{1,0:T(8,128)(2,1)}, u16[128,2048]{1,0:T(8,128)(2,1)S(1)}, u32[]{:S(2)}) copy-start(u16[128,2048]{1,0:T(8,128)(2,1)S(1)} %get-tuple-element.265) | copy-start | bytes 1572868 | tf_op jit(solution)/shard_map/while
  186.1 2.7 %copy-start.12 = (bf16[2,128,16,128]{3,2,1,0:T(8,128)(2,1)S(1)}, bf16[2,128,16,128]{3,2,1,0:T(8,128)(2,1)}, u32[]{:S(2)}) copy-start(bf16[2,128,16,128]{3,2,1,0:T(8,128)(2,1)} %get-tuple-element.298) | copy-start | bytes 3145732 | tf_op jit(solution)/shard_map/while
  189.2 1.0 copy-start.13
  207.9 14.6 %copy-start.10 = (s32[8]{0:T(128)S(1)}, s32[8]{0:T(128)}, u32[]{:S(2)}) copy-start(s32[8]{0:T(128)} %get-tuple-element.135) | copy-start | bytes 100
  208.6 13.8 %all-to-all-start.2 = ((bf16[8,1,128,128]{3,2,1,0:T(8,128)(2,1)}), bf16[8,1,128,128]{3,2,1,0:T(8,128)(2,1)S(1)}, u32[]{:S(2)}, u32[]{:S(2)}) async-start(bf16[8,1,128,128]{3,2,1,0:T(8,128)(2,1)} %fusion.39), calls=%async_computation.2 | async-start | bytes 524288 | tf_op jit(solution)/shard_map/all_to_all | solution.py:137
  213.9 40.2 %all-reduce.6.cloned.1.call-start = ((), (), s32[]{:S(2)}) async-start(), calls=%async_computation.4 | async-start | bytes 131072 | tf_op jit(solution)/shard_map/psum | solution.py:149
Sparse Core Ops, SparseCore 0:
  48.0 49.9 all-reduce.3
  224.3 29.7 all-reduce.5
where the time goes:
time: 265 us; the launch traced here: 264 us
  waiting for transfers between devices  94.7 us (36%)
  other arithmetic  40.9 us (15%)
  blocking collectives  39.5 us (15%)
  matrix products  35.8 us (14%)
  between operations  18.6 us (7%)
  local copies, waits for them, and re-layouts  17.7 us (7%)
  starting transfers between devices  16 us (6%)
    psum x1, waiting for transfers between devices, local(): score_part = lax.psum(partial_value, 'head')  46.2 us
    psum x1, blocking collectives, local(): lax.psum((loss_part, is_first * pair_local), ('seq', 'head'))  39.5 us
    psum x1, waiting for transfers between devices, local(): lax.psum(owned_grad.astype(jnp.bfloat16), 'head').astype(jnp.float32)  28 us
    dot_general x4, matrix products, dot_values(): jnp.einsum('qhd,kd->qhk', query_tile, key_tile.reshape(-1, key_width), pr...  19.5 us
    reduce_sum x2, other arithmetic, backward(): jnp.sum(jnp.maximum(values, 0.0) * grad_tile[:, None, :], axis=2)  14.9 us
    dot_general x2, matrix products, backward(): jnp.einsum('qhk,qhd->kd', dot_grads, query_tile, preferred_element_type=j...  10.9 us
    all_to_all x1, waiting for transfers between devices, local(): lax.all_to_all(spread[tiles_here:].reshape(owner_count, CAP, BLOCK, key_w...  8.45 us
    all_to_all x1, waiting for transfers between devices, local(): lax.all_to_all(reply_blocks, 'seq', split_axis=0, concat_axis=0, tiled=True)  7.99 us
  transfers between devices with their start and end apart: 5, of which 5 were waited for; matrix products, arithmetic and copies ran while one was open for 2% of the time, Pallas kernels for 0%

commit v1 on v0

--- a/solution.py
+++ b/solution.py
@@ -86,7 +86,8 @@
     partial_value = lax.map(forward, (query_tiles, weight_tiles, fetched)).reshape(row_count, KEYS)
     target_vals = jnp.where(live_mask, targets.astype(jnp.float32), 0.0)
     pair_local = jnp.sum(live_mask.astype(jnp.float32))
-    score_part = lax.psum(partial_value, "head")
+    parts = lax.all_gather(partial_value, "head", axis=0, tiled=False)
+    score_part = parts.sum(axis=0)
     row_max, row_norm, row_target = row_statistics(score_part, live_mask, target_vals)
     target_prob = jnp.where(live_mask, target_vals / row_target[:, None], 0.0)
     kl_cols = jnp.sum(

time: 265 us -> 274 us (1.034)
  waiting for transfers between devices: 94.7 us -> 102 us
    all_gather x0 -> x1, waiting for transfers between devices: none -> 53.1 us  [local(): parts = lax.all_gather(partial_value, 'head', axis=0, tiled=False)]
    psum x1 -> x0, waiting for transfers between devices: 46.2 us -> none  [local(): score_part = lax.psum(partial_value, 'head')]
    reduce_sum x0 -> x1, other arithmetic: none -> 4.4 us  [local(): score_part = parts.sum(axis=0)]
where the time goes in v1:
time: 274 us; the launch traced here: 273 us
  waiting for transfers between devices  102 us (37%)
  other arithmetic  43.4 us (16%)
  blocking collectives  39.4 us (14%)
  matrix products  35.8 us (13%)
  between operations  18.5 us (7%)
  local copies, waits for them, and re-layouts  17.9 us (7%)
  starting transfers between devices  16 us (6%)
    all_gather x1, waiting for transfers between devices, local(): parts = lax.all_gather(partial_value, 'head', axis=0, tiled=False)  53.1 us
    psum x1, blocking collectives, local(): lax.psum((loss_part, is_first * pair_local), ('seq', 'head'))  39.4 us
    psum x1, waiting for transfers between devices, local(): lax.psum(owned_grad.astype(jnp.bfloat16), 'head').astype(jnp.float32)  28.1 us
    dot_general x4, matrix products, dot_values(): jnp.einsum('qhd,kd->qhk', query_tile, key_tile.reshape(-1, key_width), pr...  19.5 us
    reduce_sum x2, other arithmetic, backward(): jnp.sum(jnp.maximum(values, 0.0) * grad_tile[:, None, :], axis=2)  14.9 us
    dot_general x2, matrix products, backward(): jnp.einsum('qhk,qhd->kd', dot_grads, query_tile, preferred_element_type=j...  10.9 us
    all_to_all x1, waiting for transfers between devices, local(): lax.all_to_all(spread[tiles_here:].reshape(owner_count, CAP, BLOCK, key_w...  8.47 us
    all_to_all x1, waiting for transfers between devices, local(): lax.all_to_all(reply_blocks, 'seq', split_axis=0, concat_axis=0, tiled=True)  7.99 us
  transfers between devices with their start and end apart: 5, of which 5 were waited for; matrix products, arithmetic and copies ran while one was open for 2% of the time, Pallas kernels for 0%

profile of v1, /device:TPU:0, one launch (start us, length us, event | category | flops | bytes accessed | tf_op | source)
XLA Modules:
  0.0 273.0 jit_solution(12194441531059110639)
XLA Ops:
  7.2 0.8 select_reduce_fusion.2
  7.9 0.7 broadcast_maximum_fusion
  8.7 0.7 gather_fusion
  9.5 0.7 and_select_fusion.3
  10.8 0.7 copy.39
  11.5 7.3 %all-to-all-start = ((s32[8,1,1]{2,1,0:T(1,128)}), s32[8,1,1]{2,1,0:T(1,128)S(1)}, u32[]{:S(2)}, u32[]{:S(2)}) async-start(s32[8,1,1]{2,1,0:T(1,128)} %copy.39), calls=%async_computation | async-start | bytes 8192 | tf_op jit(solution)/shard_map/all_to_all | solution.py:57
  18.8 1.5 copy.42
  20.4 0.7 gather_fusion.2
  21.2 4.0 %all-to-all-done = s32[8,1,1]{2,1,0:T(1,128)S(1)} async-done(((s32[8,1,1]{2,1,0:T(1,128)}), s32[8,1,1]{2,1,0:T(1,128)S(1)}, u32[]{:S(2)}, u32[]{:S(2)}) %all-to-all-start) | async-done | bytes 64 | tf_op jit(solution)/shard_map/all_to_all | solution.py:57
  25.2 0.7 fusion.46
  25.9 1.3 gather_fusion.1
  27.2 3.4 %all-to-all-start.1 = ((bf16[8,1,128,128]{3,2,1,0:T(8,128)(2,1)}), bf16[8,1,128,128]{3,2,1,0:T(8,128)(2,1)S(1)}, u32[]{:S(2)}, u32[]{:S(2)}) async-start(bf16[8,1,128,128]{3,2,1,0:T(8,128)(2,1)} %bitcast.22), calls=%async_computation.1 | async-start | bytes 524288 | tf_op jit(solution)/shard_map/all_to_all | solution.py:59
  30.8 8.0 %all-to-all-done.1 = bf16[8,1,128,128]{3,2,1,0:T(8,128)(2,1)S(1)} async-done(((bf16[8,1,128,128]{3,2,1,0:T(8,128)(2,1)}), bf16[8,1,128,128]{3,2,1,0:T(8,128)(2,1)S(1)}, u32[]{:S(2)}, u32[]{:S(2)}) %all-to-all-start.1) | async-done | bytes 262176 | tf_op jit(solution)/shard_map/all_to_all | solution.py:59
  38.8 0.7 gather_fusion.3
  39.6 8.5 %while.24 = (s32[]{:T(128)}, f32[2,128,2048]{2,1,0:T(8,128)}, bf16[2,128,16,128]{3,1,2,0:T(8,128)(2,1)S(1)}, bf16[2,16,128,128]{3,2,1,0:T(8,128)(2,1)S(1)}, f32[2,128,16]{1,2,0:T(8,128)S(1)}, /*index=5*/s32[]{:T(128)}) while((s32[]{:T(128)}, f32[2,128,2048]{2,1,0:T(8,128)}, bf16[2,128,16,128]{3,1,2,0:T(8,128)(2,1)S(1)}, ...), condition=%wide.region_6.7_spmd, body=%wide.region_4.6_spmd.sunk | while | flops 1086324736 | bytes 22044820 | solution.py:86
  39.7 2.6 multiply_reduce_fusion.4
  42.4 1.4 copy-done.6
  43.9 2.6 multiply_reduce_fusion.4
  46.7 1.4 copy-done.6
  48.9 1.3 convert_reduce_fusion
  50.8 1.2 or_and_fusion
  52.0 53.1 %all-gather.2.cloned.1.call-done = f32[4,256,2048]{2,1,0:T(8,128)} async-done(((f32[1,256,2048]{2,1,0:T(8,128)}), f32[4,256,2048]{2,1,0:T(8,128)}) %all-gather.2.cloned.1.call-update) | async-done | bytes 8388624 | tf_op jit(solution)/shard_map/all_gather | solution.py:89
  105.1 4.4 %reduce_sum.92 = f32[256,2048]{1,0:T(8,128)S(1)} reduce(f32[4,256,2048]{2,1,0:T(8,128)} %all-gather.2.cloned.1.call-done, f32[]{:T(128)} %constant.68.clone.1), dimensions={0}, to_apply=%region_7.8 | reduce | flops 1572864 | bytes 10485764 | tf_op jit(solution)/shard_map/reduce_sum | solution.py:90
  109.5 2.2 select_reduce_fusion.1
  111.7 2.4 select_reduce_fusion
  116.5 39.4 %all-reduce = (f32[]{:T(128)}, f32[]{:T(128)}) all-reduce(f32[]{:T(128)S(6)} %mul.105, f32[]{:T(128)S(6)} %mul.107), channel_id=1, replica_groups=mesh['seq'=8,'head'=4] {'seq','head'}, use_global_device_ids=true, to_apply=%region_12.13 | all-reduce | flops 2 | bytes 16 | tf_op jit(solution)/shard_map/psum | solution.py:102
  156.0 4.7 %multiply_divide_fusion = f32[256,2048]{1,0:T(8,128)} fusion(f32[256,2048]{1,0:T(8,128)S(1)} %reduce_sum.92, bf16[256,2048]{1,0:T(8,128)(2,1)} %param.13, f32[]{:T(128)} %get-tuple-element.163, f32[256]{0:T(256)S(1)} %get-tuple-element.134, f32[256]{0:T(256)S(1)} %get-tuple-element.132, f32[256]{0:T(256)S(1)} %get-tuple-element.133, ...), kind=kLoop, calls=%fused_computation.50 | loop fusion | flops 5767168 | bytes 5770244 | tf_op jit(solution)/shard_map/div | solution.py:107
  160.7 51.8 %while.25 = (s32[]{:T(128)}, bf16[2,128,16,128]{3,2,1,0:T(8,128)(2,1)}, f32[2,128,16]{1,0,2:T(2,128)S(1)}, f32[2,16,128,128]{3,2,1,0:T(8,128)}, bf16[2,128,16,12...) while((s32[]{:T(128)}, ...), condition=%wide.region_15.16_spmd, body=%wide.region_13.15_spmd.sunk | while | flops 3313502208 | bytes 61949172 | solution.py:131
  160.8 1.6 dynamic-slice_bitcast_fusion.6
  162.4 7.1 %fusion.74 = (u16[128,2048]{1,0:T(8,128)(2,1)S(1)}, f32[128,16,2048]{2,0,1:T(8,128)}) fusion(bf16[2048,128,1]{1,0,2:T(8,128)(2,1)S(1)} %bitcast.147, bf16[2,128,16,128]{3,1,2,0:T(8,128)(2,1)S(1)} %copy-done.2, s32[]{:T(128)S(6)} %copy.99), kind=kOutput, calls=%fused_computation.21.clone.1 | convolution fusion | flops 1094451200 | bytes 18350084 | tf_op jit(solution)/shard_map/while/body/eval_jaxpr/qhd,kd->qhk/dot_general | solution.py:74
  169.5 2.7 fusion.75
  172.6 1.0 copy-done.13
  173.6 7.5 %multiply_reduce_fusion.5 = f32[128,16]{0,1:T(8,128)S(1)} fusion(f32[128,16,2048]{2,0,1:T(8,128)} %get-tuple-element.266, f32[128,2048]{1,0:T(8,128)S(1)} %get-tuple-element.263), kind=kLoop, calls=%fused_computation.19.clone.1 | loop fusion | flops 12580864 | bytes 17833984 | tf_op jit(solution)/shard_map/while/body/eval_jaxpr/reduce_sum | solution.py:114
  181.1 5.4 %fusion.76 = f32[2,16,128,128]{3,2,1,0:T(8,128)} fusion(f32[2,16,128,128]{3,2,1,0:T(8,128)} %get-tuple-element.300, s32[]{:T(128)S(6)} %copy.99, bf16[2,128,16,128]{3,1,2,0:T(8,128)(2,1)} %get-tuple-element.311, f32[2048,128]{0,1:T(8,128)S(1)} %get-tuple-element.267, f32[16,128]{1,0:T(8,128)S(1)} %get-tuple-element.268, u16[128,2048]{1,0:T(8,128)(2,1)} %copy-done), kind=kOutput, calls=%fused_computation.28.clone.1 | convolution fusion | flops 1103101952 | bytes 3154944 | tf_op jit(solution)/shard_map/while/body/eval_jaxpr/qhk,qhd->kd/dot_general | solution.py:126
  186.6 1.6 dynamic-slice_bitcast_fusion.6
  188.3 7.1 %fusion.74 = (u16[128,2048]{1,0:T(8,128)(2,1)S(1)}, f32[128,16,2048]{2,0,1:T(8,128)}) fusion(bf16[2048,128,1]{1,0,2:T(8,128)(2,1)S(1)} %bitcast.147, bf16[2,128,16,128]{3,1,2,0:T(8,128)(2,1)S(1)} %copy-done.2, s32[]{:T(128)S(6)} %copy.99), kind=kOutput, calls=%fused_computation.21.clone.1 | convolution fusion | flops 1094451200 | bytes 18350084 | tf_op jit(solution)/shard_map/while/body/eval_jaxpr/qhd,kd->qhk/dot_general | solution.py:74
  195.4 2.7 fusion.75
  198.5 1.0 copy-done.13
  199.5 7.5 %multiply_reduce_fusion.5 = f32[128,16]{0,1:T(8,128)S(1)} fusion(f32[128,16,2048]{2,0,1:T(8,128)} %get-tuple-element.266, f32[128,2048]{1,0:T(8,128)S(1)} %get-tuple-element.263), kind=kLoop, calls=%fused_computation.19.clone.1 | loop fusion | flops 12580864 | bytes 17833984 | tf_op jit(solution)/shard_map/while/body/eval_jaxpr/reduce_sum | solution.py:114
  207.0 5.4 %fusion.76 = f32[2,16,128,128]{3,2,1,0:T(8,128)} fusion(f32[2,16,128,128]{3,2,1,0:T(8,128)} %get-tuple-element.300, s32[]{:T(128)S(6)} %copy.99, bf16[2,128,16,128]{3,1,2,0:T(8,128)(2,1)} %get-tuple-element.311, f32[2048,128]{0,1:T(8,128)S(1)} %get-tuple-element.267, f32[16,128]{1,0:T(8,128)S(1)} %get-tuple-element.268, u16[128,2048]{1,0:T(8,128)(2,1)} %copy-done), kind=kOutput, calls=%fused_computation.28.clone.1 | convolution fusion | flops 1103101952 | bytes 3154944 | tf_op jit(solution)/shard_map/while/body/eval_jaxpr/qhk,qhd->kd/dot_general | solution.py:126
  212.5 4.7 %scatter_fusion = f32[10,128,128]{2,1,0:T(8,128)S(1)} fusion(f32[10,128,128]{2,1,0:T(8,128)S(1)} %broadcast_in_dim.106, s32[32]{0:T(128)S(1)} %copy-done.11, f32[32,128,128]{2,1,0:T(8,128)} %bitcast.155), kind=kCustom, calls=%fused_computation.4 | custom fusion | flops 524288 | bytes 6291584 | tf_op jit(solution)/shard_map/scatter-add | solution.py:135
  217.2 0.7 fusion.39
  217.9 5.3 %all-to-all-start.2 = ((bf16[8,1,128,128]{3,2,1,0:T(8,128)(2,1)}), bf16[8,1,128,128]{3,2,1,0:T(8,128)(2,1)S(1)}, u32[]{:S(2)}, u32[]{:S(2)}) async-start(bf16[8,1,128,128]{3,2,1,0:T(8,128)(2,1)} %fusion.39), calls=%async_computation.2 | async-start | bytes 524288 | tf_op jit(solution)/shard_map/all_to_all | solution.py:138
  223.3 8.5 %all-to-all-done.2 = bf16[8,1,128,128]{3,2,1,0:T(8,128)(2,1)S(1)} async-done(((bf16[8,1,128,128]{3,2,1,0:T(8,128)(2,1)}), bf16[8,1,128,128]{3,2,1,0:T(8,128)(2,1)S(1)}, u32[]{:S(2)}, u32[]{:S(2)}) %all-to-all-start.2) | async-done | bytes 262176 | tf_op jit(solution)/shard_map/all_to_all | solution.py:138
  231.8 1.0 scatter_fusion.1
  232.8 0.6 convert_element_type.35
  235.4 28.1 %all-reduce.3.cloned.1.call-done = bf16[256,128]{1,0:T(8,128)(2,1)} async-done(((bf16[256,128]{1,0:T(8,128)(2,1)}), bf16[256,128]{1,0:T(8,128)(2,1)}) %all-reduce.3.cloned.1.call-update) | async-done | bytes 65552 | tf_op jit(solution)/shard_map/psum | solution.py:150
  263.5 1.5 reshape.286
  (90 shorter events, 5.3 us)
Async XLA Ops:
  8.7 17.2 %copy-start.7 = (bf16[256,128]{1,0:T(8,128)(2,1)S(1)}, bf16[256,128]{1,0:T(8,128)(2,1)}, u32[]{:S(2)}) copy-start(bf16[256,128]{1,0:T(8,128)(2,1)} %param.12) | copy-start | bytes 196612
  11.5 13.7 %all-to-all-start = ((s32[8,1,1]{2,1,0:T(1,128)}), s32[8,1,1]{2,1,0:T(1,128)S(1)}, u32[]{:S(2)}, u32[]{:S(2)}) async-start(s32[8,1,1]{2,1,0:T(1,128)} %copy.39), calls=%async_computation | async-start | bytes 8192 | tf_op jit(solution)/shard_map/all_to_all | solution.py:57
  18.8 12.0 %copy-start.9 = (bf16[256,16]{0,1:T(8,128)(2,1)S(1)}, bf16[256,16]{0,1:T(8,128)(2,1)}, u32[]{:S(2)}) copy-start(bf16[256,16]{0,1:T(8,128)(2,1)} %param.11) | copy-start | bytes 24580
  27.2 11.6 %all-to-all-start.1 = ((bf16[8,1,128,128]{3,2,1,0:T(8,128)(2,1)}), bf16[8,1,128,128]{3,2,1,0:T(8,128)(2,1)S(1)}, u32[]{:S(2)}, u32[]{:S(2)}) async-start(bf16[8,1,128,128]{3,2,1,0:T(8,128)(2,1)} %bitcast.22), calls=%async_computation.1 | async-start | bytes 524288 | tf_op jit(solution)/shard_map/all_to_all | solution.py:59
  30.6 74.5 %all-gather.2.cloned.1.call-start = ((), (), s32[]{:S(2)}) async-start(), calls=%async_computation.3 | async-start | bytes 10485760 | tf_op jit(solution)/shard_map/all_gather | solution.py:89
  39.6 2.7 copy-start.5
  42.4 1.4 copy-start.6
  43.9 2.7 copy-start.5
  46.7 1.4 copy-start.6
  48.1 4.0 %copy-start.1 = (bf16[2,128,16,128]{3,1,2,0:T(8,128)(2,1)}, bf16[2,128,16,128]{3,1,2,0:T(8,128)(2,1)S(1)}, u32[]{:S(2)}) copy-start(bf16[2,128,16,128]{3,1,2,0:T(8,128)(2,1)S(1)} %get-tuple-element.320) | copy-start | bytes 3145732
  48.1 0.7 copy-start.14
  48.1 0.7 copy-start.8
  109.5 2.2 copy-start.3
  109.5 2.2 copy-start.4
  160.7 51.8 %copy-start.11 = (s32[32]{0:T(128)S(1)}, s32[32]{0:T(128)}, u32[]{:S(2)}) copy-start(s32[32]{0:T(128)} %reshape.323) | copy-start | bytes 388
  160.7 1.7 copy-start.2
  169.5 2.7 copy-start
  169.5 2.7 copy-start.12
  172.6 1.0 copy-start.13
  186.6 1.7 copy-start.2
  195.4 2.7 copy-start
  195.4 2.7 copy-start.12
  198.5 1.0 copy-start.13
  217.2 14.6 %copy-start.10 = (s32[8]{0:T(128)S(1)}, s32[8]{0:T(128)}, u32[]{:S(2)}) copy-start(s32[8]{0:T(128)} %get-tuple-element.135) | copy-start | bytes 100
  217.9 13.8 %all-to-all-start.2 = ((bf16[8,1,128,128]{3,2,1,0:T(8,128)(2,1)}), bf16[8,1,128,128]{3,2,1,0:T(8,128)(2,1)S(1)}, u32[]{:S(2)}, u32[]{:S(2)}) async-start(bf16[8,1,128,128]{3,2,1,0:T(8,128)(2,1)} %fusion.39), calls=%async_computation.2 | async-start | bytes 524288 | tf_op jit(solution)/shard_map/all_to_all | solution.py:138
  223.2 40.3 %all-reduce.3.cloned.1.call-start = ((), (), s32[]{:S(2)}) async-start(), calls=%async_computation.4 | async-start | bytes 131072 | tf_op jit(solution)/shard_map/psum | solution.py:150
Sparse Core Ops, SparseCore 0:
  48.2 56.8 all-gather.1
  233.6 29.8 all-reduce.2
